TPU v7x, 32 devices: a whole 2x2x4 slice. The times are simulated.
32 devices in a mesh: section: 16 (over z, y, core), dp: 2 (over x).
Axes of the slice: x: 2, y: 2, z: 4, core: 2. Of those that a mesh axis runs over, the one named last changes fastest.
Arguments:
- layer_in: bfloat16 [16, 256, 5120], P('section', 'dp'), may hold values from -6 to 6
- latent: bfloat16 [16, 256, 384], P('section', 'dp'), may hold values from -6 to 6
- mix_grad: bfloat16 [16, 256, 5120], P('section', 'dp'), may hold values from -0.375 to 0.375
- down_proj: bfloat16 [16, 5120, 384], P('section', 'dp'), may hold values from -0.078125 to 0.078125
- up_proj: bfloat16 [16, 384, 5120], P('section', None, 'dp'), may hold values from -0.3125 to 0.3125
- norm_gain: bfloat16 [16, 5120], P('section', 'dp'), may hold values from 0.5 to 1.5
- mix_weight: float32 [16, 8], P('section'), may hold values from 0.2 to 1
Outputs:
- up_grad: bfloat16 [16, 384, 5120], P('section', None, 'dp')
- down_grad: bfloat16 [16, 5120, 384], P('section', 'dp')
- gain_grad: float32 [16, 5120], P('section', 'dp')
- mixing_grad: float32 [16, 8], P('section')
All inputs are finite; a program needn't handle non-finite values.
Results may differ from a plain program's by a relative error of at most 0.0064.
Values may be sent and summed in bfloat16 or wider, within the bound.
A program may use at most 128 MiB of HBM per device.

v0:
```python
import functools

import jax
import jax.numpy as jnp
from jax import lax
from jax.experimental import pallas as pl
from jax.experimental.pallas import tpu as pltpu
from jax.sharding import PartitionSpec as P

MIXES = 8
LEVELS = MIXES // 2
REACH = LEVELS - 1
SLOTS = 2 * REACH
CHUNK = 16
TILE = 640

epsilon = 1e-06
root_coef = 0.7978845608028654
MESH = pl.DeviceIdType.MESH
F32 = jnp.float32
BF16 = jnp.bfloat16


def gelu_pair(values):
    tangent = jnp.tanh(root_coef * (values + 0.044715 * values * values * values))
    result = 0.5 * values * (1.0 + tangent)
    slopes = 0.5 * (1.0 + tangent) + 0.5 * values * (1.0 - tangent * tangent) * root_coef * (
        1.0 + 3.0 * 0.044715 * values * values
    )
    return (result, slopes)


def fold(values):
    rows, cols = values.shape
    total = jnp.sum(values.reshape(rows // 8, 8, cols), axis=0)
    out = total[:, 0:128]
    for at in range(128, cols, 128):
        out = out + total[:, at : at + 128]
    return out


def kernel(
    n, stride,
    x_ref, lat_ref, g_ref, down_ref, up_ref, gain_ref, mw_ref,
    upg_ref, dng_ref, gaing_ref, mix_ref,
    xo, cin, latv, gb, inv, actv, slopes, lown, lpeer, sacc, sout, og, mixacc,
    mst, mrecv_y, msx, mrecv_dp, wpeer, upv, downv, apart, apown, rsb, lg,
    wown, wlow, llow, lowacc, s0out, s0in, mixlow, mlow, mlowin,
    loc, gsend, grecv, xsend, xrecv, tsend, trecv, isend, irecv, wsem, zsend, zrecv,
    wlsend, wlrecv, llsend, llrecv, s0send, s0recv, mlsend, mlrecv,
    ssend, srecv, lsend, lrecv, rsend, rrecv, asend, arecv, mysem, msend, mrecv,
):
    own_rows, width = x_ref.shape
    feats = width // n
    half = own_rows // 2
    subs = half // CHUNK
    chunks = n * subs
    tiles = feats // TILE

    sec = lax.axis_index("section")
    x = lax.axis_index("dp")
    q = sec // stride
    res = sec % stride
    a = q // 2
    h = q % 2

    def at(level, side):
        return (2 * level + side) * stride + res

    me_y = sec
    other_y = at(a, 1 - h)
    above = at(a + 1, h)
    below = at(a - 1, h)

    def dev(section, dp):
        return {"section": section, "dp": dp}

    def to(k):
        return lax.rem(x + k, n)

    def source(k):
        return lax.rem(x + n - k, n)

    def remote(src, dst, ssem, rsem, section, dp):
        return pltpu.make_async_remote_copy(
            src_ref=src, dst_ref=dst, send_sem=ssem, recv_sem=rsem,
            device_id=dev(section, dp), device_id_type=MESH,
        )

    def rows(start, size, unit):
        return pl.ds(pl.multiple_of(start, unit), size)

    barrier = pltpu.get_barrier_semaphore()
    for k in range(n):
        for e in range(2):
            if k or e:
                pl.semaphore_signal(
                    barrier, inc=1, device_id=dev(other_y if e else me_y, to(k)), device_id_type=MESH
                )

    @pl.when(a > 0)
    def _():
        pl.semaphore_signal(barrier, inc=1, device_id=dev(below, x), device_id_type=MESH)

    @pl.when(a < LEVELS - 1)
    def _():
        pl.semaphore_signal(barrier, inc=1, device_id=dev(above, x), device_id_type=MESH)

    @pl.when(h == 0)
    def _():
        for slot in range(MIXES):
            wown[slot : slot + 1] = jnp.broadcast_to(mw_ref[0:1, slot : slot + 1], (1, 128))

    @pl.when(h == 1)
    def _():
        wown[0:1] = jnp.zeros((1, 128), F32)
        for slot in range(1, MIXES):
            wown[slot : slot + 1] = jnp.broadcast_to(mw_ref[0:1, slot - 1 : slot], (1, 128))

    own_cols = rows(x * feats, feats, 128)
    own_block = rows(x * own_rows, own_rows, own_rows)
    local = [
        pltpu.make_async_copy(
            g_ref.at[rows(h * half, half, half), own_cols], gb.at[h, rows(x * half, half, half)], loc.at[0]
        ),
        pltpu.make_async_copy(lat_ref, latv.at[own_block], loc.at[1]),
        pltpu.make_async_copy(x_ref, xo, loc.at[2]),
        pltpu.make_async_copy(x_ref.at[:, own_cols], cin.at[own_block], loc.at[3]),
        pltpu.make_async_copy(up_ref, upv, loc.at[4]),
        pltpu.make_async_copy(down_ref, downv, loc.at[5]),
    ]
    for copy in local:
        copy.start()

    neighbours = jnp.where(a > 0, 1, 0) + jnp.where(a < LEVELS - 1, 1, 0)
    pl.semaphore_wait(barrier, 2 * n - 1 + neighbours)

    sends = []

    def go(copy):
        copy.start()
        sends.append(copy)
        return copy

    def g_copy(k, e):
        side = 1 - h if e else h
        return remote(
            g_ref.at[rows(side * half, half, half), rows(to(k) * feats, feats, 128)],
            gb.at[h, rows(x * half, half, half)],
            gsend.at[e * n + k], grecv.at[e * n + k],
            other_y if e else me_y, to(k),
        )

    def g_arrival(k, e):
        slot = 1 - h if e else h
        dst = gb.at[slot, rows(source(k) * half, half, half)]
        return remote(dst, dst, gsend.at[e * n + k], grecv.at[e * n + k], me_y, to(k) if k else x)

    go(g_copy(0, 1))
    w_copy = go(remote(wown, wpeer, wsem.at[0], wsem.at[1], other_y, x))
    for k in range(1, n):
        go(remote(lat_ref, latv.at[own_block], tsend.at[k], trecv.at[k], me_y, to(k)))
        go(g_copy(k, 0))
        go(g_copy(k, 1))
    for k in range(1, n):
        go(remote(
            x_ref.at[:, rows(to(k) * feats, feats, 128)], cin.at[own_block],
            xsend.at[k], xrecv.at[k], me_y, to(k),
        ))

    def arrival(dst, ssem, rsem):
        return remote(dst, dst, ssem, rsem, other_y, x)

    def chunk_at(c):
        k, sub = divmod(c, subs)
        return source(k), k, sub

    def z_copy(slot, c):
        j, _, sub = chunk_at(c)
        span = rows(j * half + sub * CHUNK, CHUNK, CHUNK)
        return remote(
            gb.at[slot, span], gb.at[slot + 2, span], zsend.at[slot, c], zrecv.at[slot + 2, c], below, x
        )

    def z_arrival(slot, c):
        j, _, sub = chunk_at(c)
        dst = gb.at[slot, rows(j * half + sub * CHUNK, CHUNK, CHUNK)]
        return remote(dst, dst, zsend.at[slot - 2, c], zrecv.at[slot, c], other_y, x)

    def holds(d):
        return (a + d < LEVELS) if d == 0 else jnp.logical_and(a > 0, a + d < LEVELS)

    def flow(c):
        j, k, sub = chunk_at(c)
        if sub == 0:
            if k == 0:
                local[0].wait()
            else:
                g_arrival(k, 0).wait_recv()
            g_arrival(k, 1).wait_recv()

        @pl.when(a > 1)
        def _():
            z_copy(0, c).start()
            z_copy(1, c).start()

        for d in range(1, REACH):
            @pl.when(holds(d))
            def _():
                for slot in (2 * d, 2 * d + 1):
                    z_arrival(slot, c).wait_recv()
                    if d < REACH - 1:
                        @pl.when(a > 1)
                        def _():
                            z_copy(slot, c).start()

    def weight(ref, slot):
        return ref[slot : slot + 1, 0:1]

    def s0_copy(bb, c):
        j, _, sub = chunk_at(c)
        span = rows(j * half + sub * CHUNK, CHUNK, CHUNK)
        return remote(
            s0out.at[bb, span], s0in.at[bb, span], s0send.at[bb, c], s0recv.at[bb, c], below, x
        )

    def low_copy(bb, k):
        j = source(k)
        span = rows(j * half, half, half)
        src = lpeer.at[span] if bb else lown.at[rows(j * own_rows + h * half, half, half)]
        return remote(src, llow.at[bb, span], llsend.at[bb, k], llrecv.at[bb, k], above, x)

    def wlow_copy(bb):
        return remote(wpeer if bb else wown, wlow.at[bb], wlsend.at[bb], wlrecv.at[bb], above, x)

    def mlow_copy():
        return remote(mlow, mlowin, mlsend.at[0], mlrecv.at[0], below, x)

    def low_inner(c):
        j, k, sub = chunk_at(c)
        span = rows(j * half + sub * CHUNK, CHUNK, CHUNK)
        if sub == 0:
            for bb in range(2):
                low_copy(bb, k).wait_recv()

        @pl.loop(0, tiles)
        def _(t):
            cols = rows(t * TILE, TILE, 128)
            mine = llow[0, span, cols].astype(F32)
            theirs = llow[1, span, cols].astype(F32)
            for slot in range(SLOTS):
                values = gb[slot, span, cols].astype(F32)
                lowacc[slot + 2] += fold(values * mine)
                lowacc[8 + slot + 2] += fold(values * theirs)

    def combine(c):
        j, _, sub = chunk_at(c)
        span = rows(j * half + sub * CHUNK, CHUNK, CHUNK)
        @pl.when(a == 1)
        def _():
            @pl.loop(0, tiles)
            def _(t):
                cols = rows(t * TILE, TILE, 128)
                for bb in range(2):
                    value = jnp.zeros((CHUNK, TILE), F32)
                    for slot in range(SLOTS):
                        value = value + wlow[bb, slot + 2 : slot + 3, 0:1] * gb[slot, span, cols].astype(F32)
                    s0out[bb, span, cols] = value.astype(BF16)

            for bb in range(2):
                s0_copy(bb, c).start()

        for d in range(REACH):
            @pl.when(holds(d))
            def _():
                @pl.loop(0, tiles)
                def _(t):
                    cols = rows(t * TILE, TILE, 128)
                    first = gb[2 * d, span, cols].astype(F32)
                    second = gb[2 * d + 1, span, cols].astype(F32)
                    for bb, ref in ((0, wown), (1, wpeer)):
                        value = weight(ref, 2 * d) * first + weight(ref, 2 * d + 1) * second
                        if d:
                            value = sacc[bb, :, cols] + value
                        sacc[bb, :, cols] = value

        @pl.when(a == 0)
        def _():
            for bb in range(2):
                s0_copy(bb, c).wait_recv()

            @pl.loop(0, tiles)
            def _(t):
                cols = rows(t * TILE, TILE, 128)
                for bb in range(2):
                    sacc[bb, :, cols] += s0in[bb, span, cols].astype(F32)

        @pl.loop(0, tiles)
        def _(t):
            cols = rows(t * TILE, TILE, 128)
            og[rows(j * own_rows + h * half + sub * CHUNK, CHUNK, CHUNK), cols] = sacc[0, :, cols].astype(BF16)
            sout[span, cols] = sacc[1, :, cols].astype(BF16)

        go(remote(
            sout.at[span], og.at[rows(j * own_rows + h * half + sub * CHUNK, CHUNK, CHUNK)],
            ssend.at[c], srecv.at[c], other_y, x,
        ))

    def s_arrival(c):
        j, _, sub = chunk_at(c)
        return arrival(
            og.at[rows(j * own_rows + (1 - h) * half + sub * CHUNK, CHUNK, CHUNK)], ssend.at[c], srecv.at[c]
        )

    def inner(c):
        j, k, sub = chunk_at(c)
        span = rows(j * half + sub * CHUNK, CHUNK, CHUNK)
        own_span = rows(j * own_rows + h * half + sub * CHUNK, CHUNK, CHUNK)
        if sub == 0:
            arrival(lpeer.at[rows(j * half, half, half)], lsend.at[k], lrecv.at[k]).wait_recv()

            @pl.when(a == 0)
            def _():
                low_copy(1, k).start()
        for d in range(REACH):
            @pl.when(holds(d))
            def _():
                @pl.loop(0, tiles)
                def _(t):
                    cols = rows(t * TILE, TILE, 128)
                    mine = lown[own_span, cols].astype(F32)
                    theirs = lpeer[span, cols].astype(F32)
                    for slot in (2 * d, 2 * d + 1):
                        values = gb[slot, span, cols].astype(F32)
                        mixacc[slot] += fold(values * mine)
                        mixacc[8 + slot] += fold(values * theirs)

    mixacc[...] = jnp.zeros_like(mixacc)
    lowacc[...] = jnp.zeros_like(lowacc)
    local[2].wait()

    def square(t, total):
        part = xo[:, rows(t * TILE, TILE, 128)].astype(F32)
        part = part * part
        for at_col in range(0, TILE, 128):
            total = total + part[:, at_col : at_col + 128]
        return total

    lanes = lax.fori_loop(0, width // TILE, square, jnp.zeros((own_rows, 128), F32))
    mean_sq = jnp.sum(lanes, axis=1, keepdims=True) / width
    inv[own_block] = jnp.broadcast_to(lax.rsqrt(mean_sq + epsilon), (own_rows, 128))
    for k in range(1, n):
        go(remote(inv.at[own_block], inv.at[own_block], isend.at[k], irecv.at[k], me_y, to(k)))

    arrival(wpeer, wsem.at[0], wsem.at[1]).wait_recv()

    @pl.when(a == 0)
    def _():
        for bb in range(2):
            wlow_copy(bb).start()

    flow(0)

    local[1].wait()
    for k in range(1, n):
        arrival(latv.at[rows(source(k) * own_rows, own_rows, own_rows)], tsend.at[k], trecv.at[k]).wait_recv()
    _, own_slopes = gelu_pair(latv[own_block].astype(F32))
    slopes[...] = own_slopes
    for j in range(n):
        block = slice(j * own_rows, (j + 1) * own_rows)
        values, _ = gelu_pair(latv[block].astype(F32))
        actv[block] = values.astype(BF16)
    local[4].wait()
    local[3].wait()

    def layer_out(k):
        j = source(k)
        block = rows(j * own_rows, own_rows, own_rows)
        if k:
            arrival(cin.at[block], xsend.at[k], xrecv.at[k]).wait_recv()

        @pl.loop(0, tiles)
        def _(t):
            cols = rows(t * TILE, TILE, 128)
            branch = jnp.dot(actv[block, :], upv[:, cols], preferred_element_type=F32)
            lown[block, cols] = (cin[block, cols].astype(F32) + branch).astype(BF16)

        go(remote(
            lown.at[rows(j * own_rows + (1 - h) * half, half, half)], lpeer.at[rows(j * half, half, half)],
            lsend.at[k], lrecv.at[k], other_y, x,
        ))

        @pl.when(a == 0)
        def _():
            low_copy(0, k).start()

    def act_block(k):
        j = source(k)
        for sub in range(subs):
            s_arrival(k * subs + sub).wait_recv()
        part = lax.dot_general(
            og[rows(j * own_rows, own_rows, own_rows), :], upv[...], (((1,), (1,)), ((), ())),
            preferred_element_type=F32,
        )
        if k == 0:
            apown[...] = part
        else:
            apart[k] = part.astype(BF16)
            go(remote(apart.at[k], rsb.at[k], rsend.at[k], rrecv.at[k], me_y, j))

    layer_out(0)

    @pl.when(a == 1)
    def _():
        for bb in range(2):
            wlow_copy(bb).wait_recv()

    combine(0)
    for c in range(1, chunks):
        k, sub = divmod(c, subs)
        flow(c)
        combine(c)
        inner(c - 1)
        if sub == 0:
            layer_out(k)
            act_block(k - 1)
        if c >= subs:
            @pl.when(a == 1)
            def _():
                low_inner(c - subs)
    inner(chunks - 1)
    act_block(n - 1)

    @pl.when(a == 1)
    def _():
        for c in range(chunks - subs, chunks):
            low_inner(c)
        for bb in range(2):
            for slot in range(8):
                mlow[bb, slot : slot + 1] = jnp.sum(lowacc[8 * bb + slot], axis=0, keepdims=True)
        mlow_copy().start()

    for bb in range(2):
        for slot in range(8):
            mst[bb, slot : slot + 1] = jnp.sum(mixacc[8 * bb + slot], axis=0, keepdims=True)

    @pl.loop(0, tiles)
    def _(t):
        cols = rows(t * TILE, TILE, 128)
        upg_ref[:, cols] = lax.dot_general(
            actv[...], og[:, cols], (((0,), (0,)), ((), ())), preferred_element_type=F32
        ).astype(BF16)


    total = apown[...]
    for k in range(1, n):
        arrival(rsb.at[k], rsend.at[k], rrecv.at[k]).wait_recv()
        total = total + rsb[k].astype(F32)
    lg[own_block] = (total * slopes[...]).astype(BF16)
    for k in range(1, n):
        go(remote(lg.at[own_block], lg.at[own_block], asend.at[k], arecv.at[k], me_y, to(k)))

    mixlow[...] = jnp.zeros_like(mixlow)

    @pl.when(a == 0)
    def _():
        mlow_copy().wait_recv()
        mixlow[...] = mlowin[...]

    mst[...] = mst[...] + mixlow[...]
    go(remote(mst.at[1], mrecv_y, mysem.at[0], mysem.at[1], other_y, x))
    for k in range(1, n):
        block = rows(source(k) * own_rows, own_rows, own_rows)
        arrival(inv.at[block], isend.at[k], irecv.at[k]).wait_recv()
        arrival(lg.at[block], asend.at[k], arecv.at[k]).wait_recv()
    local[5].wait()

    arrival(mrecv_y, mysem.at[0], mysem.at[1]).wait_recv()
    msx[...] = mst[0] + mrecv_y[...]
    for k in range(1, n):
        go(remote(msx, mrecv_dp.at[k], msend.at[k], mrecv.at[k], me_y, to(k)))

    @pl.loop(0, tiles)
    def _(t):
        cols = rows(t * TILE, TILE, 128)
        scaled = cin[:, cols].astype(F32) * inv[:, 0:1]
        normed = (scaled * gain_ref[:, cols].astype(F32)).astype(BF16)
        dng_ref[rows(t * TILE, TILE, 128), :] = lax.dot_general(
            normed, lg[...], (((0,), (0,)), ((), ())), preferred_element_type=F32
        ).astype(BF16)
        norm_grad = lax.dot_general(
            lg[...], downv[rows(t * TILE, TILE, 128), :], (((1,), (1,)), ((), ())),
            preferred_element_type=F32,
        )
        gaing_ref[:, cols] = jnp.sum(norm_grad * scaled, axis=0, keepdims=True)

    mixed = msx[...]
    for k in range(1, n):
        arrival(mrecv_dp.at[k], msend.at[k], mrecv.at[k]).wait_recv()
        mixed = mixed + mrecv_dp[k]
    sums = jnp.sum(mixed, axis=1, keepdims=True)
    lane = lax.broadcasted_iota(jnp.int32, (1, MIXES), 1)

    def mix_row(shift):
        row = jnp.zeros((1, MIXES), F32)
        for m in range(MIXES - shift):
            row = jnp.where(lane == m, sums[m + shift : m + shift + 1, 0:1], row)
        mix_ref[...] = row

    @pl.when(h == 0)
    def _():
        mix_row(0)

    @pl.when(h == 1)
    def _():
        mix_row(1)

    for copy in sends:
        copy.wait_send()

    @pl.when(a > 1)
    def _():
        for c in range(chunks):
            z_copy(0, c).wait_send()
            z_copy(1, c).wait_send()

    for d in range(1, REACH - 1):
        @pl.when(jnp.logical_and(a > 1, a + d < LEVELS))
        def _():
            for c in range(chunks):
                z_copy(2 * d, c).wait_send()
                z_copy(2 * d + 1, c).wait_send()

    @pl.when(a == 1)
    def _():
        mlow_copy().wait_send()
        for c in range(chunks):
            for bb in range(2):
                s0_copy(bb, c).wait_send()

    @pl.when(a == 0)
    def _():
        for bb in range(2):
            wlow_copy(bb).wait_send()
            for k in range(n):
                low_copy(bb, k).wait_send()


def local(layer_in, latent, mix_grad, down_proj, up_proj, norm_gain, mix_weight):
    _, own_rows, width = layer_in.shape
    n = lax.axis_size("dp")
    stride = lax.axis_size("section") // MIXES
    latents = latent.shape[2]
    feats = width // n
    tokens = own_rows * n
    chunks = tokens // 2 // CHUNK
    dma = pltpu.SemaphoreType.DMA
    anyspace = pl.BlockSpec(memory_space=pl.ANY)
    vmem = pl.BlockSpec(memory_space=pltpu.VMEM)
    up_grad, down_grad, gain_grad, mixed = pl.pallas_call(
        functools.partial(kernel, n, stride),
        out_shape=(
            jax.ShapeDtypeStruct((latents, feats), BF16),
            jax.ShapeDtypeStruct((feats, latents), BF16),
            jax.ShapeDtypeStruct((1, feats), F32),
            jax.ShapeDtypeStruct((1, MIXES), F32),
        ),
        in_specs=[anyspace] * 5 + [vmem] * 2,
        out_specs=(vmem,) * 4,
        scratch_shapes=[
            pltpu.VMEM((own_rows, width), BF16),
            pltpu.VMEM((tokens, feats), BF16),
            pltpu.VMEM((tokens, latents), BF16),
            pltpu.VMEM((SLOTS, tokens // 2, feats), BF16),
            pltpu.VMEM((tokens, 128), F32),
            pltpu.VMEM((tokens, latents), BF16),
            pltpu.VMEM((own_rows, latents), F32),
            pltpu.VMEM((tokens, feats), BF16),
            pltpu.VMEM((tokens // 2, feats), BF16),
            pltpu.VMEM((2, CHUNK, feats), F32),
            pltpu.VMEM((tokens // 2, feats), BF16),
            pltpu.VMEM((tokens, feats), BF16),
            pltpu.VMEM((16, 8, 128), F32),
            pltpu.VMEM((2, 8, 128), F32),
            pltpu.VMEM((8, 128), F32),
            pltpu.VMEM((8, 128), F32),
            pltpu.VMEM((n, 8, 128), F32),
            pltpu.VMEM((8, 128), F32),
            pltpu.VMEM((latents, feats), BF16),
            pltpu.VMEM((feats, latents), BF16),
            pltpu.VMEM((n, own_rows, latents), BF16),
            pltpu.VMEM((own_rows, latents), F32),
            pltpu.VMEM((n, own_rows, latents), BF16),
            pltpu.VMEM((tokens, latents), BF16),
            pltpu.VMEM((8, 128), F32),
            pltpu.VMEM((2, 8, 128), F32),
            pltpu.VMEM((2, tokens // 2, feats), BF16),
            pltpu.VMEM((16, 8, 128), F32),
            pltpu.VMEM((2, tokens // 2, feats), BF16),
            pltpu.VMEM((2, tokens // 2, feats), BF16),
            pltpu.VMEM((2, 8, 128), F32),
            pltpu.VMEM((2, 8, 128), F32),
            pltpu.VMEM((2, 8, 128), F32),
            dma((6,)),
            dma((2 * n,)), dma((2 * n,)),
            dma((n,)), dma((n,)),
            dma((n,)), dma((n,)),
            dma((n,)), dma((n,)),
            dma((2,)),
            dma((SLOTS, chunks)), dma((SLOTS, chunks)),
            dma((2,)), dma((2,)),
            dma((2, n)), dma((2, n)),
            dma((2, chunks)), dma((2, chunks)),
            dma((1,)), dma((1,)),
            dma((chunks,)), dma((chunks,)),
            dma((n,)), dma((n,)),
            dma((n,)), dma((n,)),
            dma((n,)), dma((n,)),
            dma((2,)),
            dma((n,)), dma((n,)),
        ],
        compiler_params=pltpu.CompilerParams(
            collective_id=0, has_side_effects=True, vmem_limit_bytes=60 * 1024 * 1024
        ),
    )(layer_in[0], latent[0], mix_grad[0], down_proj[0], up_proj[0], norm_gain, mix_weight)
    return (up_grad[None], down_grad[None], gain_grad, mixed)


def solution(mesh):
    return jax.shard_map(
        local,
        mesh=mesh,
        in_specs=(
            P("section", "dp", None),
            P("section", "dp", None),
            P("section", "dp", None),
            P("section", "dp", None),
            P("section", None, "dp"),
            P("section", "dp"),
            P("section", None),
        ),
        out_specs=(
            P("section", None, "dp"),
            P("section", "dp", None),
            P("section", "dp"),
            P("section", None),
        ),
        check_vma=False,
    )
```

profile of v0, /device:TPU:0, one launch (start us, length us, event | category | flops | bytes accessed | tf_op | source)
XLA Modules:
  0.0 103.8 jit_solution(17557750706710934651)
XLA Ops:
  0.6 97.6 %shard_map.102 = (bf16[384,2560]{1,0:T(8,128)(2,1)}, bf16[2560,384]{1,0:T(8,128)(2,1)}, f32[1,2560]{1,0:T(1,128)}, f32[1,8]{1,0:T(1,128)}) custom-call(bf16[128,5120]{1,0:T(8,128)(2,1)} %bitcast.11, bf16[128,384]{1,0:T(8,128)(2,1)} %bitcast.13, bf16[128,5120]{1,0:T(8,128)(2,1)} %bitcast.12, bf16[2560,384]{1,0:T(8,128)(2,1)} %bitcast.7, ...), custom_call_target="tpu_custom_call" | custom-call | tf_op jit(solution)/shard_map/pallas_call | solution.py:560
  98.3 0.0 copy-start
  98.3 3.1 %copy.15 = bf16[1,384,2560]{2,1,0:T(8,128)(2,1)} copy(bf16[1,384,2560]{2,1,0:T(8,128)(2,1)} %bitcast.10) | data formatting | bytes 3932160
  101.4 0.0 copy-done
  101.4 0.0 copy-start.1
  101.4 0.0 copy-start.2
  101.4 1.3 %copy.16 = bf16[1,2560,384]{2,1,0:T(8,128)(2,1)} copy(bf16[1,2560,384]{2,1,0:T(8,128)(2,1)S(1)} %bitcast.9) | data formatting | bytes 3932160
  102.7 0.0 copy-done.1
  102.7 0.6 copy.17
  103.3 0.0 copy-done.2
  103.3 0.5 copy.18
Async XLA Ops:
  98.3 3.1 %copy-start = (bf16[2560,384]{1,0:T(8,128)(2,1)S(1)}, bf16[2560,384]{1,0:T(8,128)(2,1)}, u32[]{:S(2)}) copy-start(bf16[2560,384]{1,0:T(8,128)(2,1)} %get-tuple-element.9) | copy-start | bytes 5898244
  101.4 1.3 %copy-start.1 = (f32[1,2560]{1,0:T(1,128)S(1)}, f32[1,2560]{1,0:T(1,128)}, u32[]{:S(2)}) copy-start(f32[1,2560]{1,0:T(1,128)} %get-tuple-element.18) | copy-start | bytes 30724
  101.4 1.9 %copy-start.2 = (f32[1,8]{1,0:T(1,128)S(1)}, f32[1,8]{1,0:T(1,128)}, u32[]{:S(2)}) copy-start(f32[1,8]{1,0:T(1,128)} %get-tuple-element.19) | copy-start | bytes 100
where the time goes:
time: 104 us
  Pallas kernels  97.6 us (94%)
  local copies, waits for them, and re-layouts  5.48 us (5%)
    pallas_call x1, Pallas kernels, local(): pl.pallas_call(functools.partial(kernel, n, stride), out_shape=(jax.Shape...  97.6 us
    unnamed x10, local copies, waits for them, and re-layouts  5.48 us

commit v1 on v0

v1 whole, which is shorter than its diff:
```python
import functools

import jax
import jax.numpy as jnp
from jax import lax
from jax.experimental import pallas as pl
from jax.experimental.pallas import tpu as pltpu
from jax.sharding import PartitionSpec as P

MIXES = 8
LEVELS = MIXES // 2
SLOTS = 6
CHUNK = 16
TILE = 640

epsilon = 1e-06
root_coef = 0.7978845608028654
MESH = pl.DeviceIdType.MESH
F32 = jnp.float32
BF16 = jnp.bfloat16
DMA = pltpu.SemaphoreType.DMA


def gelu_pair(values):
    tangent = jnp.tanh(root_coef * (values + 0.044715 * values * values * values))
    result = 0.5 * values * (1.0 + tangent)
    slopes = 0.5 * (1.0 + tangent) + 0.5 * values * (1.0 - tangent * tangent) * root_coef * (
        1.0 + 3.0 * 0.044715 * values * values
    )
    return (result, slopes)


def fold(values):
    rows, cols = values.shape
    total = jnp.sum(values.reshape(rows // 8, 8, cols), axis=0)
    out = total[:, 0:128]
    for at in range(128, cols, 128):
        out = out + total[:, at : at + 128]
    return out


def rows(start, size, unit):
    return pl.ds(pl.multiple_of(start, unit), size)


def scratch(n, own_rows, width, latents):
    feats = width // n
    tokens = own_rows * n
    half = tokens // 2
    chunks = half // CHUNK
    return dict(
        xo=pltpu.VMEM((own_rows, width), BF16),
        cin=pltpu.VMEM((tokens, feats), BF16),
        latv=pltpu.VMEM((tokens, latents), BF16),
        gb=pltpu.VMEM((SLOTS, half, feats), BF16),
        gq=pltpu.VMEM((2, tokens, feats), BF16),
        inv=pltpu.VMEM((tokens, 128), F32),
        actv=pltpu.VMEM((tokens, latents), BF16),
        actt=pltpu.VMEM((latents, tokens), BF16),
        slopes=pltpu.VMEM((tokens, latents), F32),
        lown=pltpu.VMEM((tokens, feats), BF16),
        lpeer=pltpu.VMEM((half, feats), BF16),
        llow=pltpu.VMEM((2, half, feats), BF16),
        sacc=pltpu.VMEM((4, half, feats), F32),
        sout=pltpu.VMEM((3, half, feats), BF16),
        s0in=pltpu.VMEM((tokens, feats), BF16),
        og=pltpu.VMEM((tokens, feats), BF16),
        acc=pltpu.VMEM((4 * MIXES, 8, 128), F32),
        wall=pltpu.VMEM((4, MIXES, 128), F32),
        mst=pltpu.VMEM((4, MIXES, 128), F32),
        mtot=pltpu.VMEM((MIXES, 128), F32),
        mixin=pltpu.VMEM((2, 2, n, MIXES, 128), F32),
        upv=pltpu.VMEM((latents, feats), BF16),
        apown=pltpu.VMEM((tokens, latents), F32),
        apart=pltpu.VMEM((tokens, latents), BF16),
        rsb=pltpu.VMEM((n, tokens, latents), BF16),
        loc=DMA((6,)),
        gsend=DMA((2, chunks)), grecv=DMA((2, chunks)),
        qsend=DMA((2, n)), qrecv=DMA((2, n)),
        xsend=DMA((n,)), xrecv=DMA((n,)),
        tsend=DMA((n,)), trecv=DMA((n,)),
        isend=DMA((n,)), irecv=DMA((n,)),
        wsend=DMA((4,)), wrecv=DMA((4,)),
        zsend=DMA((4, chunks)), zrecv=DMA((SLOTS, chunks)),
        lsend=DMA((n,)), lrecv=DMA((n,)),
        usend=DMA((2, n)), urecv=DMA((2, n)),
        ssend=DMA((3, chunks)), srecv=DMA((3, chunks)),
        rsend=DMA((n, n)), rrecv=DMA((n, n)),
        msend=DMA((2, 2, n)), mrecv=DMA((2, 2, n)),
    )


def exchange(
    n, stride, names,
    x_ref, lat_ref, g_ref, down_ref, up_ref, gain_ref, mw_ref,
    upg_ref, nt_ref, lg_ref, downv, mix_ref,
    *refs,
):
    s = type("Scratch", (), dict(zip(names, refs)))
    xo, cin, latv, gb, gq, inv = s.xo, s.cin, s.latv, s.gb, s.gq, s.inv
    actv, lown, lpeer, llow, sacc, sout = s.actv, s.lown, s.lpeer, s.llow, s.sacc, s.sout
    s0in, og, acc, wall, mst, mtot, mixin, upv = s.s0in, s.og, s.acc, s.wall, s.mst, s.mtot, s.mixin, s.upv
    own_rows, width = x_ref.shape
    feats = width // n
    half = own_rows // 2
    subs = half // CHUNK
    chunks = n * subs
    tiles = feats // TILE

    sec = lax.axis_index("section")
    x = lax.axis_index("dp")
    q = sec // stride
    res = sec % stride
    a = q // 2
    h = q % 2
    o = 1 - h

    def at(level, side):
        return (2 * level + side) * stride + res

    def to(k):
        return lax.rem(x + k, n) if k else x

    def source(k):
        return lax.rem(x + n - k, n) if k else x

    def remote(src, dst, ssem, rsem, section, dp):
        return pltpu.make_async_remote_copy(
            src_ref=src, dst_ref=dst, send_sem=ssem, recv_sem=rsem,
            device_id={"section": section, "dp": dp}, device_id_type=MESH,
        )

    def arrival(dst, rsem):
        return remote(dst, dst, rsem, rsem, at(a, o), x)

    barrier = pltpu.get_barrier_semaphore()

    def greet(section, dp):
        pl.semaphore_signal(
            barrier, inc=1, device_id={"section": section, "dp": dp}, device_id_type=MESH
        )

    for e in range(2):
        for k in range(n):
            if k or e:
                greet(at(a, o if e else h), to(k))

    @pl.when(a == 0)
    def _():
        for e in range(2):
            for k in range(n):
                greet(at(1, o if e else h), to(k))

    @pl.when(a == 1)
    def _():
        for e in range(2):
            for k in range(n):
                greet(at(0, o if e else h), to(k))
        greet(at(2, h), x)

    @pl.when(a == 2)
    def _():
        greet(at(1, h), x)
        greet(at(3, h), x)

    @pl.when(a == 3)
    def _():
        greet(at(2, h), x)

    own_cols = rows(x * feats, feats, 128)
    own_block = rows(x * own_rows, own_rows, own_rows)
    local = [
        pltpu.make_async_copy(x_ref, xo, s.loc.at[0]),
        pltpu.make_async_copy(lat_ref, latv.at[own_block], s.loc.at[1]),
        pltpu.make_async_copy(x_ref.at[:, own_cols], cin.at[own_block], s.loc.at[2]),
        pltpu.make_async_copy(up_ref, upv, s.loc.at[3]),
        pltpu.make_async_copy(down_ref, downv, s.loc.at[4]),
    ]
    for copy in local:
        copy.start()

    def g_local():
        return pltpu.make_async_copy(
            g_ref.at[rows(h * half, half, half), own_cols], gb.at[h, rows(x * half, half, half)], s.loc.at[5]
        )

    def q_local():
        return pltpu.make_async_copy(g_ref.at[:, own_cols], gq.at[h, own_block], s.loc.at[5])

    @pl.when(a > 0)
    def _():
        g_local().start()

    @pl.when(a == 0)
    def _():
        q_local().start()

    @pl.when(h == 0)
    def _():
        for slot in range(MIXES):
            wall[0, slot : slot + 1] = jnp.broadcast_to(mw_ref[0:1, slot : slot + 1], (1, 128))

    @pl.when(h == 1)
    def _():
        wall[0, 0:1] = jnp.zeros((1, 128), F32)
        for slot in range(1, MIXES):
            wall[0, slot : slot + 1] = jnp.broadcast_to(mw_ref[0:1, slot - 1 : slot], (1, 128))

    met = 2 * n - 1 + jnp.where(a < 2, 2 * n, 0) + jnp.where(a == 2, 2, jnp.where(a == 0, 0, 1))
    pl.semaphore_wait(barrier, met)

    sends = {level: [] for level in range(LEVELS)}

    def go(level, make, *args):
        make(*args).start()
        sends[level].append(functools.partial(make, *args))

    def chunk_at(c):
        k, sub = divmod(c, subs)
        return source(k), k, sub

    def span(c):
        j, _, sub = chunk_at(c)
        return rows(j * half + sub * CHUNK, CHUNK, CHUNK)

    def wide(c, side):
        j, _, sub = chunk_at(c)
        return rows(j * own_rows + side * half + sub * CHUNK, CHUNK, CHUNK)

    def g_copy(e, c):
        k, sub = divmod(c, subs)
        side = o if e else h
        return remote(
            g_ref.at[rows(side * half + sub * CHUNK, CHUNK, CHUNK), rows(to(k) * feats, feats, 128)],
            gb.at[h, rows(x * half + sub * CHUNK, CHUNK, CHUNK)],
            s.gsend.at[e, c], s.grecv.at[e, c], at(a, side), to(k),
        )

    def g_wait(e, c):
        arrival(gb.at[o if e else h, span(c)], s.grecv.at[e, c]).wait_recv()

    def q_send(e, k):
        return remote(
            g_ref.at[:, rows(to(k) * feats, feats, 128)], gq.at[h, own_block],
            s.qsend.at[e, k], s.qrecv.at[e, k], at(a, o if e else h), to(k),
        )

    def q_wait(e, k):
        block = rows(source(k) * own_rows, own_rows, own_rows)
        arrival(gq.at[o if e else h, block], s.qrecv.at[e, k]).wait_recv()

    def x_copy(k):
        return remote(
            x_ref.at[:, rows(to(k) * feats, feats, 128)], cin.at[own_block],
            s.xsend.at[k], s.xrecv.at[k], at(a, h), to(k),
        )

    def z_copy(e, c, relay):
        k, sub = divmod(c, subs)
        slot = (o if e else h) + (2 if relay else 0)
        if not relay and not e and not k:
            src = g_ref.at[rows(h * half + sub * CHUNK, CHUNK, CHUNK), own_cols]
        else:
            src = gb.at[slot, span(c)]
        lane = e + (2 if relay else 0)
        return remote(
            src, gb.at[slot + 2, span(c)], s.zsend.at[lane, c], s.zrecv.at[lane + 2, c],
            at(a - 1, h), x,
        )

    def z_wait(e, c, deep):
        slot = (o if e else h) + (4 if deep else 2)
        arrival(gb.at[slot, span(c)], s.zrecv.at[e + (4 if deep else 2), c]).wait_recv()

    def w_copy():
        return remote(wall.at[0], wall.at[1], s.wsend.at[1], s.wrecv.at[1], at(a, o), x)

    def w_low(e):
        return remote(
            wall.at[0], wall.at[2 + e], s.wsend.at[2 + e], s.wrecv.at[2 + e], at(1, o if e else h), x
        )

    def square():
        local[0].wait()

        def step(t, total):
            part = xo[:, rows(t * TILE, TILE, 128)].astype(F32)
            part = part * part
            for at_col in range(0, TILE, 128):
                total = total + part[:, at_col : at_col + 128]
            return total

        lanes = lax.fori_loop(0, width // TILE, step, jnp.zeros((own_rows, 128), F32))
        mean_sq = jnp.sum(lanes, axis=1, keepdims=True) / width
        inv[own_block] = jnp.broadcast_to(lax.rsqrt(mean_sq + epsilon), (own_rows, 128))

    def inv_copy(k):
        return remote(
            inv.at[own_block], inv.at[own_block], s.isend.at[k], s.irecv.at[k], at(a, h), to(k)
        )

    def inv_send(level):
        for k in range(1, n):
            go(level, inv_copy, k)

    def lat_copy(k):
        return remote(
            lat_ref, latv.at[own_block], s.tsend.at[k], s.trecv.at[k], at(a, h), to(k)
        )

    def gelu(k):
        block = rows(source(k) * own_rows, own_rows, own_rows)
        if k:
            arrival(latv.at[block], s.trecv.at[k]).wait_recv()
        else:
            local[1].wait()
        values, slopes = gelu_pair(latv[block].astype(F32))
        actv[block] = values.astype(BF16)
        s.slopes[block] = slopes

    def layer_out(k):
        block = rows(source(k) * own_rows, own_rows, own_rows)
        if k:
            arrival(cin.at[block], s.xrecv.at[k]).wait_recv()
        else:
            local[2].wait()
            local[3].wait()

        @pl.loop(0, tiles)
        def _(t):
            cols = rows(t * TILE, TILE, 128)
            branch = jnp.dot(actv[block, :], upv[:, cols], preferred_element_type=F32)
            lown[block, cols] = (cin[block, cols].astype(F32) + branch).astype(BF16)

    def l_copy(k):
        j = source(k)
        return remote(
            lown.at[rows(j * own_rows + o * half, half, half)], lpeer.at[rows(j * half, half, half)],
            s.lsend.at[k], s.lrecv.at[k], at(a, o), x,
        )

    def l_wait(k):
        arrival(lpeer.at[rows(source(k) * half, half, half)], s.lrecv.at[k]).wait_recv()

    def up_copy(e, k):
        j = source(k)
        block = rows(j * half, half, half)
        src = lpeer.at[block] if e else lown.at[rows(j * own_rows + h * half, half, half)]
        return remote(src, llow.at[e, block], s.usend.at[e, k], s.urecv.at[e, k], at(1, h), x)

    def up_wait(k):
        for e in range(2):
            arrival(llow.at[e, rows(source(k) * half, half, half)], s.urecv.at[e, k]).wait_recv()

    def weight(target, slot):
        slot = slot + 2 if target > 1 else slot
        return wall[target, slot : slot + 1, 0:1]

    def add(c, slots, targets, first, final):
        here = span(c)
        mine = wide(c, h)

        @pl.loop(0, tiles)
        def _(t):
            cols = rows(t * TILE, TILE, 128)
            parts = [gb[slot, here, cols].astype(F32) for slot in slots]
            for target in range(targets):
                value = None if first else sacc[target, here, cols]
                for slot, part in zip(slots, parts):
                    term = weight(target, slot) * part
                    value = term if value is None else value + term
                if not final:
                    sacc[target, here, cols] = value
                elif target == 0:
                    og[mine, cols] = value.astype(BF16)
                else:
                    sout[target - 1, here, cols] = value.astype(BF16)

    def s_copy(c):
        return remote(
            sout.at[0, span(c)], og.at[wide(c, h)], s.ssend.at[0, c], s.srecv.at[0, c], at(a, o), x
        )

    def s0_copy(e, c):
        return remote(
            sout.at[1 + e, span(c)], s0in.at[wide(c, h)], s.ssend.at[1 + e, c], s.srecv.at[1 + e, c],
            at(0, o if e else h), x,
        )

    def s_wait(c):
        arrival(og.at[wide(c, o)], s.srecv.at[0, c]).wait_recv()

    def s0_wait(c):
        for e in range(2):
            arrival(s0in.at[wide(c, o if e else h)], s.srecv.at[1 + e, c]).wait_recv()

    def inner(c, slots, targets):
        here = span(c)
        mine = wide(c, h)

        @pl.loop(0, tiles)
        def _(t):
            cols = rows(t * TILE, TILE, 128)
            parts = [gb[slot, here, cols].astype(F32) for slot in slots]
            for target in range(targets):
                if target == 0:
                    other = lown[mine, cols]
                elif target == 1:
                    other = lpeer[here, cols]
                else:
                    other = llow[target - 2, here, cols]
                other = other.astype(F32)
                for slot, part in zip(slots, parts):
                    place = MIXES * target + (slot + 2 if target > 1 else slot)
                    acc[place] += fold(part * other)

    def mix_parts(targets):
        for target in range(targets):
            for slot in range(MIXES):
                mst[target, slot : slot + 1] = jnp.sum(acc[MIXES * target + slot], axis=0, keepdims=True)

    def mix_copy(target, k):
        low, e = divmod(target, 2)
        return remote(
            mst.at[target], mixin.at[low, e, k], s.msend.at[low, e, k], s.mrecv.at[low, e, k],
            at(0 if low else a, o if e else h), to(k),
        )

    def mix_send(target, level):
        for k in range(n):
            if k or target:
                go(level, mix_copy, target, k)

    def mix_take(low, e):
        for k in range(n):
            if k or low or e:
                arrival(mixin.at[low, e, k], s.mrecv.at[low, e, k]).wait_recv()
                mtot[...] += mixin[low, e, k]

    def act_block(k):
        j = source(k)
        block = rows(j * own_rows, own_rows, own_rows)
        part = lax.dot_general(
            og[block, :], upv[...], (((1,), (1,)), ((), ())), preferred_element_type=F32,
        )
        s.apown[block] = part
        s.apart[block] = part.astype(BF16)

    def act_copy(d, k):
        block = rows(source(k) * own_rows, own_rows, own_rows)
        return remote(
            s.apart.at[block], s.rsb.at[d, block], s.rsend.at[d, k], s.rrecv.at[d, k], at(a, h), to(d)
        )

    def act_send(k, level):
        for d in range(1, n):
            go(level, act_copy, d, k)

    def normed():
        for k in range(1, n):
            block = rows(source(k) * own_rows, own_rows, own_rows)
            arrival(inv.at[block], s.irecv.at[k]).wait_recv()

        @pl.loop(0, tiles)
        def _(t):
            cols = rows(t * TILE, TILE, 128)
            scaled = cin[:, cols].astype(F32) * inv[:, 0:1]
            normed = (scaled * gain_ref[:, cols].astype(F32)).astype(BF16)
            nt_ref[rows(t * TILE, TILE, 128), :] = normed.T

    def begin():
        acc[...] = jnp.zeros_like(acc)
        square()
        gelu(0)

    def middle():
        for k in range(1, n):
            gelu(k)
        s.actt[...] = actv[...].T

    def first_sends(level):
        go(level, w_copy)
        for k in range(1, n):
            go(level, lat_copy, k)

    def w_take():
        arrival(wall.at[1], s.wrecv.at[1]).wait_recv()

    def spread(level, x_first):
        for sub in range(subs):
            go(level, g_copy, 1, sub)
        if x_first:
            for k in range(1, n):
                go(level, x_copy, k)
        for k in range(1, n):
            for e in range(2):
                for sub in range(subs):
                    go(level, g_copy, e, k * subs + sub)
        if not x_first:
            for k in range(1, n):
                go(level, x_copy, k)

    near = (0, 1)

    def own_take(k):
        for sub in range(subs):
            c = k * subs + sub
            for e in range(2):
                if k or e:
                    g_wait(e, c)
        if k == 0:
            g_local().wait()

    @pl.when(a == 3)
    def _():
        L = 3
        for sub in range(subs):
            go(L, z_copy, 0, sub, False)
        first_sends(L)
        spread(L, False)
        begin()
        inv_send(L)
        layer_out(0)
        go(L, l_copy, 0)
        for sub in range(subs):
            g_wait(1, sub)
            go(L, z_copy, 1, sub, False)
        g_local().wait()
        for k in range(1, n):
            for e in range(2):
                for sub in range(subs):
                    g_wait(e, k * subs + sub)
                    go(L, z_copy, e, k * subs + sub, False)
        w_take()
        for c in range(chunks):
            add(c, near, 2, True, True)
            go(L, s_copy, c)
        middle()
        for k in range(1, n):
            layer_out(k)
            go(L, l_copy, k)
        normed()
        for k in range(n):
            l_wait(k)
            for sub in range(subs):
                inner(k * subs + sub, near, 2)
        mix_parts(2)
        mix_send(0, L)
        mix_send(1, L)
        for k in range(n):
            for sub in range(subs):
                s_wait(k * subs + sub)
            act_block(k)
            act_send(k, L)

    @pl.when(a == 2)
    def _():
        L = 2
        for sub in range(subs):
            go(L, z_copy, 0, sub, False)
        first_sends(L)
        spread(L, False)
        begin()
        inv_send(L)
        for sub in range(subs):
            g_wait(1, sub)
            go(L, z_copy, 1, sub, False)
        g_local().wait()
        layer_out(0)
        go(L, l_copy, 0)
        w_take()
        for k in range(1, n):
            for e in range(2):
                for sub in range(subs):
                    g_wait(e, k * subs + sub)
                    go(L, z_copy, e, k * subs + sub, False)
        for k in range(n):
            for sub in range(subs):
                c = k * subs + sub
                for e in range(2):
                    z_wait(e, c, False)
                    go(L, z_copy, e, c, True)
                add(c, (0, 1, 2, 3), 2, True, True)
                go(L, s_copy, c)
        middle()
        for k in range(1, n):
            layer_out(k)
            go(L, l_copy, k)
        normed()
        for k in range(n):
            l_wait(k)
            for sub in range(subs):
                inner(k * subs + sub, (0, 1, 2, 3), 2)
        mix_parts(2)
        mix_send(0, L)
        mix_send(1, L)
        for k in range(n):
            for sub in range(subs):
                s_wait(k * subs + sub)
            act_block(k)
            act_send(k, L)

    @pl.when(a == 1)
    def _():
        L = 1
        first_sends(L)
        spread(L, True)
        begin()
        inv_send(L)
        layer_out(0)
        go(L, l_copy, 0)
        w_take()
        for e in range(2):
            arrival(wall.at[2 + e], s.wrecv.at[2 + e]).wait_recv()
        own_take(0)
        for sub in range(subs):
            add(sub, near, 4, True, False)
        middle()
        for k in range(1, n):
            layer_out(k)
            go(L, l_copy, k)
        for sub in range(subs):
            for e in range(2):
                z_wait(e, sub, False)
            add(sub, (2, 3), 4, False, False)
        normed()
        l_wait(0)
        up_wait(0)
        for sub in range(subs):
            inner(sub, (0, 1, 2, 3), 4)
        for k in range(1, n):
            own_take(k)
            for sub in range(subs):
                c = k * subs + sub
                for e in range(2):
                    z_wait(e, c, False)
                add(c, (0, 1, 2, 3), 4, True, False)
        todo = []
        for c in range(chunks):
            for e in range(2):
                z_wait(e, c, True)
            add(c, (4, 5), 4, False, True)
            for e in range(2):
                go(L, s0_copy, e, c)
            go(L, s_copy, c)
            k, sub = divmod(c, subs)
            if k and sub == 0:
                for s2 in range(subs):
                    s_wait((k - 1) * subs + s2)
                act_block(k - 1)
                act_send(k - 1, L)
            if k and sub == subs - 2:
                l_wait(k)
                up_wait(k)
                for late in todo:
                    inner(late, (0, 1, 2, 3, 4, 5), 4)
                todo = []
            if k == 0:
                inner(c, (4, 5), 4)
            elif sub >= subs - 2:
                inner(c, (0, 1, 2, 3, 4, 5), 4)
            else:
                todo.append(c)
        mix_parts(4)
        for target in range(4):
            mix_send(target, L)
        k = n - 1
        for sub in range(subs):
            s_wait(k * subs + sub)
        act_block(k)
        act_send(k, L)

    @pl.when(a == 0)
    def _():
        L = 0
        first_sends(L)
        for e in range(2):
            go(L, w_low, e)

        @pl.when(h == 1)
        def _():
            q_send(1, 0).start()

        for k in range(1, n):
            go(L, x_copy, k)
        for k in range(1, n):
            go(L, q_send, 0, k)
        begin()
        inv_send(L)
        layer_out(0)
        go(L, l_copy, 0)
        go(L, up_copy, 0, 0)

        @pl.when(h == 1)
        def _():
            for k in range(1, n):
                q_send(1, k).start()

        w_take()
        middle()
        l_wait(0)
        go(L, up_copy, 1, 0)
        for k in range(1, n):
            layer_out(k)
            go(L, l_copy, k)
            go(L, up_copy, 0, k)
            l_wait(k)
            go(L, up_copy, 1, k)
        normed()
        q_local().wait()
        for k in range(1, n):
            q_wait(0, k)

        @pl.when(h == 0)
        def _():
            for k in range(n):
                q_wait(1, k)

        def whole_inner(slot):
            @pl.loop(0, n * own_rows // CHUNK)
            def _(c):
                here = rows(c * CHUNK, CHUNK, CHUNK)

                @pl.loop(0, tiles)
                def _(t):
                    cols = rows(t * TILE, TILE, 128)
                    acc[slot] += fold(gq[slot, here, cols].astype(F32) * lown[here, cols].astype(F32))

        whole_inner(1)

        @pl.when(h == 0)
        def _():
            whole_inner(0)

        mix_parts(1)
        mix_send(0, L)

        def finish(c, slots):
            @pl.loop(0, tiles)
            def _(t):
                cols = rows(t * TILE, TILE, 128)
                for side in (h, o):
                    here = wide(c, side)
                    value = s0in[here, cols].astype(F32)
                    for slot in slots:
                        value = value + weight(0, slot) * gq[slot, here, cols].astype(F32)
                    og[here, cols] = value.astype(BF16)

        for c in range(chunks):
            s0_wait(c)

            @pl.when(h == 0)
            def _():
                finish(c, (0, 1))

            @pl.when(h == 1)
            def _():
                finish(c, (1,))

            k, sub = divmod(c, subs)
            if sub == subs - 1:
                act_block(k)
                act_send(k, L)

    @pl.loop(0, tiles)
    def _(t):
        cols = rows(t * TILE, TILE, 128)
        upg_ref[:, cols] = jnp.dot(s.actt[...], og[:, cols], preferred_element_type=F32).astype(BF16)

    mtot[...] = mst[0]

    @pl.when(a > 0)
    def _():
        mix_take(0, 0)
        mix_take(0, 1)

    @pl.when(a == 0)
    def _():
        mix_take(0, 0)
        mix_take(1, 0)
        mix_take(1, 1)

    sums = jnp.sum(mtot[...], axis=1, keepdims=True)
    lane = lax.broadcasted_iota(jnp.int32, (1, MIXES), 1)

    def mix_row(shift):
        row = jnp.zeros((1, MIXES), F32)
        for m in range(MIXES - shift):
            row = jnp.where(lane == m, sums[m + shift : m + shift + 1, 0:1], row)
        mix_ref[...] = row

    @pl.when(h == 0)
    def _():
        mix_row(0)

    @pl.when(h == 1)
    def _():
        mix_row(1)

    local[4].wait()
    for k in range(n):
        block = rows(source(k) * own_rows, own_rows, own_rows)
        total = s.apown[block]
        for d in range(1, n):
            arrival(s.rsb.at[d, block], s.rrecv.at[d, (k - d) % n]).wait_recv()
            total = total + s.rsb[d, block].astype(F32)
        lg_ref[block] = (total * s.slopes[block]).astype(BF16)

    for level in range(LEVELS):
        @pl.when(a == level)
        def _():
            for make in sends[level]:
                make().wait_send()

    @pl.when(jnp.logical_and(a == 0, h == 1))
    def _():
        for k in range(n):
            q_send(1, k).wait_send()


def finish(
    upg_ref, nt_ref, lg_ref, down_ref, mix_ref, gain_ref,
    upo_ref, dno_ref, gaino_ref, mixo_ref, dn, sems,
):
    feats, latents = down_ref.shape
    out = [pltpu.make_async_copy(upg_ref, upo_ref, sems.at[0])]
    out[0].start()
    mixo_ref[...] = mix_ref[...]
    for t in range(feats // TILE):
        here = slice(t * TILE, (t + 1) * TILE)
        grad = jnp.dot(nt_ref[here, :], lg_ref[...], preferred_element_type=F32)
        dn[here, :] = grad.astype(BF16)
        copy = pltpu.make_async_copy(dn.at[here], dno_ref.at[here], sems.at[1 + t])
        copy.start()
        out.append(copy)
        prod = grad * down_ref[here, :].astype(F32)
        lanes = prod[:, 0:128]
        for at in range(128, latents, 128):
            lanes = lanes + prod[:, at : at + 128]
        for b in range(TILE // 128):
            cols = slice(t * TILE + b * 128, t * TILE + (b + 1) * 128)
            row = jnp.sum(lanes[b * 128 : (b + 1) * 128, :].T, axis=0, keepdims=True)
            gaino_ref[:, cols] = row / gain_ref[:, cols].astype(F32)
    for copy in out:
        copy.wait()


def local(layer_in, latent, mix_grad, down_proj, up_proj, norm_gain, mix_weight):
    _, own_rows, width = layer_in.shape
    n = lax.axis_size("dp")
    stride = lax.axis_size("section") // MIXES
    latents = latent.shape[2]
    feats = width // n
    tokens = own_rows * n
    anyspace = pl.BlockSpec(memory_space=pl.ANY)
    vmem = pl.BlockSpec(memory_space=pltpu.VMEM)
    space = scratch(n, own_rows, width, latents)
    held = pl.pallas_call(
        functools.partial(exchange, n, stride, tuple(space)),
        out_shape=(
            pltpu.VMEM((latents, feats), BF16),
            pltpu.VMEM((feats, tokens), BF16),
            pltpu.VMEM((tokens, latents), BF16),
            pltpu.VMEM((feats, latents), BF16),
            pltpu.VMEM((1, MIXES), F32),
        ),
        in_specs=[anyspace] * 5 + [vmem] * 2,
        out_specs=(vmem,) * 5,
        scratch_shapes=list(space.values()),
        compiler_params=pltpu.CompilerParams(
            collective_id=0, has_side_effects=True, vmem_limit_bytes=48 * 1024 * 1024
        ),
        name="exchange",
    )(layer_in[0], latent[0], mix_grad[0], down_proj[0], up_proj[0], norm_gain, mix_weight)
    up_grad, down_grad, gain_grad, mixed = pl.pallas_call(
        finish,
        out_shape=(
            jax.ShapeDtypeStruct((latents, feats), BF16),
            jax.ShapeDtypeStruct((feats, latents), BF16),
            jax.ShapeDtypeStruct((1, feats), F32),
            jax.ShapeDtypeStruct((1, MIXES), F32),
        ),
        in_specs=[vmem] * 6,
        out_specs=(anyspace, anyspace, vmem, vmem),
        scratch_shapes=[pltpu.VMEM((feats, latents), BF16), DMA((1 + feats // TILE,))],
        compiler_params=pltpu.CompilerParams(vmem_limit_bytes=12 * 1024 * 1024),
        name="finish",
    )(*held, norm_gain)
    return (up_grad[None], down_grad[None], gain_grad, mixed)


def solution(mesh):
    return jax.shard_map(
        local,
        mesh=mesh,
        in_specs=(
            P("section", "dp", None),
            P("section", "dp", None),
            P("section", "dp", None),
            P("section", "dp", None),
            P("section", None, "dp"),
            P("section", "dp"),
            P("section", None),
        ),
        out_specs=(
            P("section", None, "dp"),
            P("section", "dp", None),
            P("section", "dp"),
            P("section", None),
        ),
        check_vma=False,
    )
```

time: 104 us -> 85.2 us (0.82)
  Pallas kernels: 97.6 us -> 82.1 us
  local copies, waits for them, and re-layouts: 5.48 us -> 2.24 us
    pallas_call x1 -> x2, Pallas kernels: 97.6 us -> 82.1 us  [the longest x1 79.4 us: local(): pl.pallas_call(functools.partial(exchange, n, stride, tuple(space)), out_...]
    unnamed x10 -> x6, local copies, waits for them, and re-layouts: 5.48 us -> 2.24 us
where the time goes in v1:
time: 85.2 us; the launch traced here: 85 us
  Pallas kernels  82.1 us (96%)
  local copies, waits for them, and re-layouts  2.24 us (3%)
    pallas_call x1, Pallas kernels, local(): pl.pallas_call(functools.partial(exchange, n, stride, tuple(space)), out_...  79.4 us
    pallas_call x1, Pallas kernels, local(): pl.pallas_call(finish, out_shape=(jax.ShapeDtypeStruct((latents, feats),...  2.64 us
    unnamed x6, local copies, waits for them, and re-layouts  2.24 us

profile of v1, /device:TPU:0, one launch (start us, length us, event | category | flops | bytes accessed | tf_op | source)
XLA Modules:
  0.0 85.0 jit_solution(10686792720124336928)
XLA Ops:
  0.6 0.0 copy-start
  0.6 0.9 %copy-done = bf16[1,128,384]{2,1,0:T(8,128)(2,1)S(1)} copy-done((bf16[1,128,384]{2,1,0:T(8,128)(2,1)S(1)}, bf16[1,128,384]{2,1,0:T(8,128)(2,1)}, u32[]{:S(2)}) %copy-start) | copy-done | bytes 98328
  1.5 0.0 copy-start.1
  1.5 0.7 copy-done.1
  2.2 0.0 copy-start.2
  2.2 0.7 copy-done.2
  2.9 79.4 %exchange.1 = (bf16[384,2560]{1,0:T(8,128)(2,1)S(1)}, bf16[2560,256]{1,0:T(8,128)(2,1)S(1)}, bf16[256,384]{1,0:T(8,128)(2,1)S(1)}, bf16[2560,384]{1,0:T(8,128)(2,1)S(1)}, f32[1,8]{1,0:T(1,128)S(1)}) custom-call(bf16[128,5120]{1,0:T(8,128)(2,1)} %bitcast.10, bf16[128,384]{1,0:T(8,128)(2,1)S(1)} %bitcast.7, bf16[128,5120]{1,0:T(8,128)(2,1)} %bitcast.11, ...), custom_call_target="tpu_custom_call" | custom-call | tf_op jit(solution)/shard_map/exchange/pallas_call | solution.py:858
  82.3 2.6 %finish.1 = (bf16[384,2560]{1,0:T(8,128)(2,1)}, bf16[2560,384]{1,0:T(8,128)(2,1)}, f32[1,2560]{1,0:T(1,128)}, f32[1,8]{1,0:T(1,128)}) custom-call(bf16[384,2560]{1,0:T(8,128)(2,1)S(1)} %get-tuple-element.13.upg_ref, bf16[2560,256]{1,0:T(8,128)(2,1)S(1)} %get-tuple-element.14.nt_ref, bf16[256,384]{1,0:T(8,128)(2,1)S(1)} %get-tuple-element.15.lg_ref, ...), custom_call_target="tpu_custom_call" | custom-call | tf_op jit(solution)/shard_map/finish/pallas_call | solution.py:875
Async XLA Ops:
  0.6 0.9 %copy-start = (bf16[1,128,384]{2,1,0:T(8,128)(2,1)S(1)}, bf16[1,128,384]{2,1,0:T(8,128)(2,1)}, u32[]{:S(2)}) copy-start(bf16[1,128,384]{2,1,0:T(8,128)(2,1)} %param.8) | copy-start | bytes 294916
  1.5 0.7 copy-start.1
  2.2 0.7 copy-start.2
